TPU v7x, 256 devices: a whole 4x4x8 slice. The times are simulated.
256 devices in a mesh: expert: 64 (over x, z, core), mp: 4 (over y).
Axes of the slice: x: 4, y: 4, z: 8, core: 2. Of those that a mesh axis runs over, the one named last changes fastest.
Arguments:
- tokens: bfloat16 [1536, 6144], P('expert', 'mp'), may hold values from -6 to 6
- mix_weights: float32 [1536, 2], P('expert'), may hold values from 0.2 to 1
- routes: int32 [1536, 2], P('expert'), may hold values from 0 to 7, as said below
- w_gate: bfloat16 [64, 6144, 1024], P('expert', None, 'mp'), may hold values from -0.078125 to 0.078125
- w_up: bfloat16 [64, 6144, 1024], P('expert', None, 'mp'), may hold values from -0.078125 to 0.078125
- w_down: bfloat16 [64, 1024, 6144], P('expert', 'mp'), may hold values from -0.0625 to 0.0625
Outputs:
- mixed_out: bfloat16 [1536, 6144], P('expert', 'mp')
Inputs may be any that keep to these rules, and one draw needn't show every extreme that they name: `routes`: each row names 2 different experts, and every expert is named by some row. Among the 24 rows of one index of the expert axis no expert is named more than 12 times, and on some indices one is named exactly 12 times.
All inputs are finite; a program needn't handle non-finite values.
Results may differ from a plain program's by a relative error of at most 0.011.
Values may be sent and summed in bfloat16 or wider, within the bound.
No kernel may reach another device: no remote copies, remote signals or barrier semaphores. Data moves between devices by JAX's collectives and lax.ppermute only.
A program may use at most 128 MiB of HBM per device.

v0:
```python
import jax
import jax.numpy as jnp
from jax import lax
from jax.sharding import Mesh
from jax.sharding import PartitionSpec as P

EXPERTS = 8
TOP = 2
EXPERT = ("expert_0", "expert_1", "expert_2")


def joined_along(pieces, dim):
    shape = list(pieces.shape[1:])
    shape[dim] *= pieces.shape[0]
    return jnp.moveaxis(pieces, 0, dim).reshape(shape)


def copy_for_each(value, axis):
    size = lax.axis_size(axis)
    return lax.all_to_all(
        jnp.broadcast_to(value[None], (size, *value.shape)), axis, 0, 0, tiled=True
    )


def collect(value, axis, dim):
    return joined_along(copy_for_each(value, axis), dim)


def split_up(value, dim, size):
    shape = value.shape
    pieces = value.reshape(*shape[:dim], size, shape[dim] // size, *shape[dim + 1 :])
    return jnp.moveaxis(pieces, dim, 0)


def exchange_in_order(pieces, axes, sequence):
    shape = [lax.axis_size(a) for a in axes]
    pieces = pieces.reshape(*shape, *pieces.shape[1:])
    for k in sequence:
        pieces = lax.all_to_all(pieces, axes[k], split_axis=k, concat_axis=k, tiled=True)
    return pieces.reshape(-1, *pieces.shape[len(axes) :])


def exchange_by_chip(value, groups, sequence, split_dim, concat_dim):
    size = lax.axis_size(groups[0]) * lax.axis_size(groups[1])
    pieces = split_up(value, split_dim, size)
    return joined_along(exchange_in_order(pieces, groups, sequence), concat_dim)


def pack_rows(pick_tokens, features, repeats):
    packed = jnp.einsum(
        "tem,tc->emc", pick_tokens, features, preferred_element_type=jnp.float32
    ).astype(jnp.bfloat16)
    spread = jnp.broadcast_to(packed[:, None], (packed.shape[0], repeats) + packed.shape[1:])
    return spread.reshape((packed.shape[0] * repeats,) + packed.shape[1:])


def activate(gate_act, up_act):
    return (jax.nn.silu(gate_act) * up_act).astype(jnp.bfloat16)


def local(tokens, mix_weights, routes, w_gate, w_up, w_down):
    tok_rows = tokens.shape[0]
    senders = lax.axis_size(EXPERT)
    group_size = senders // EXPERTS
    capacity = 5 * tok_rows * senders * TOP // (4 * EXPERTS)
    most_rows = tok_rows // 2
    labels = jnp.arange(EXPERTS, dtype=jnp.int32)
    flat_ids = routes.reshape(-1)
    marked = (flat_ids[:, None] == labels[None, :]).astype(jnp.int32)
    earlier = jnp.cumsum(marked, axis=0) - marked
    local_rank = jnp.sum(earlier * marked, axis=1)
    counts = jnp.sum(marked, axis=0)
    count_grid = collect(counts[None, :], EXPERT, 0)
    my_index = lax.axis_index(EXPERT)
    sender_ids = jnp.arange(senders, dtype=jnp.int32)
    lower_mask = (sender_ids[:, None] < my_index).astype(jnp.int32)
    offsets = jnp.sum(count_grid * lower_mask, axis=0)
    slot_ids = jnp.sum(marked * offsets[None, :], axis=1) + local_rank
    keep_mask = (slot_ids < capacity).astype(jnp.int32)
    rank_hit = (local_rank[:, None] == jnp.arange(most_rows, dtype=jnp.int32)[None, :]).astype(
        jnp.int32
    ) * keep_mask[:, None]
    assign_pick = marked[:, :, None] * rank_hit[:, None, :]
    pick_tokens = jnp.sum(assign_pick.reshape(tok_rows, TOP, EXPERTS, most_rows), axis=1).astype(
        jnp.bfloat16
    )
    weighted = assign_pick.astype(jnp.float32) * mix_weights.reshape(-1)[:, None, None]
    combine_w = jnp.sum(weighted.reshape(tok_rows, TOP, EXPERTS * most_rows), axis=1)
    gate_rows = w_gate[0]
    up_rows = w_up[0]
    down_rows = w_down[0]
    arrived = lax.all_to_all(
        pack_rows(pick_tokens, tokens, group_size), EXPERT, split_axis=0, concat_axis=0, tiled=True
    )
    arrived_rows = arrived.reshape(senders * most_rows, arrived.shape[2])
    my_expert = my_index // group_size
    column_counts = jnp.sum(count_grid * (labels[None, :] == my_expert).astype(jnp.int32), axis=1)
    starts = jnp.cumsum(column_counts) - column_counts
    slot_pos = jnp.arange(capacity, dtype=jnp.int32)
    slot_ends = starts + column_counts
    source_of = jnp.minimum(
        jnp.sum((slot_ends[None, :] <= slot_pos[:, None]).astype(jnp.int32), axis=1), senders - 1
    )
    source_hit = (sender_ids[None, :] == source_of[:, None]).astype(jnp.int32)
    start_of = jnp.sum(source_hit * starts[None, :], axis=1)
    slot_valid = slot_pos < jnp.sum(column_counts)
    fetch_idx = jnp.where(slot_valid, source_of * most_rows + slot_pos - start_of, 0)
    in_rows = jnp.where(
        slot_valid[:, None], jnp.take(arrived_rows, fetch_idx, axis=0), jnp.zeros((), jnp.bfloat16)
    )
    shard_piece = lax.all_gather(in_rows, "mp", axis=1, tiled=True)
    gate_act = jnp.dot(shard_piece, gate_rows, preferred_element_type=jnp.float32)
    up_act = jnp.dot(shard_piece, up_rows, preferred_element_type=jnp.float32)
    hidden = activate(gate_act, up_act)
    part_sum = jnp.dot(hidden, down_rows, preferred_element_type=jnp.float32)
    reduced = lax.psum_scatter(part_sum.astype(jnp.bfloat16), "mp", scatter_dimension=1, tiled=True)
    out_width = reduced.shape[1]
    buffer_pos = jnp.arange(most_rows, dtype=jnp.int32)
    slot_back = starts[:, None] + buffer_pos[None, :]
    back_valid = (buffer_pos[None, :] < column_counts[:, None]) & (slot_back < capacity)
    back_idx = jnp.where(back_valid, slot_back, 0).reshape(-1)
    back_rows = jnp.where(
        back_valid.reshape(-1)[:, None],
        jnp.take(reduced, back_idx, axis=0),
        jnp.zeros((), jnp.bfloat16),
    )
    returned = exchange_by_chip(
        back_rows.reshape(senders, most_rows, out_width),
        (("expert_0", "expert_1"), "expert_2"),
        (1, 0),
        0,
        0,
    )
    summed = jnp.sum(
        returned.reshape(EXPERTS, group_size, most_rows, out_width).astype(jnp.float32), axis=1
    )
    result = jnp.dot(
        combine_w, summed.reshape(EXPERTS * most_rows, out_width), precision=lax.Precision.HIGHEST
    )
    return result.astype(jnp.bfloat16)


def solution(mesh):
    torus = Mesh(
        mesh.devices.reshape(4, 8, 2, mesh.shape["mp"]), ("expert_0", "expert_1", "expert_2", "mp")
    )
    placed = (
        P(EXPERT, "mp"),
        P(EXPERT, None),
        P(EXPERT, None),
        P(EXPERT, None, "mp"),
        P(EXPERT, None, "mp"),
        P(EXPERT, "mp", None),
    )
    return jax.shard_map(
        local, mesh=torus, in_specs=placed, out_specs=P(EXPERT, "mp"), check_vma=False
    )
```

profile of v0, /device:TPU:6, one launch (start us, length us, event | category | flops | bytes accessed | tf_op | source)
XLA Modules:
  0.0 377.2 jit_solution(595688700204690243)
XLA Ops:
  6.5 0.9 copy.54
  8.3 12.2 %all-to-all-start = ((s32[64,1,8]{2,1,0:T(1,128)}), s32[64,1,8]{2,1,0:T(1,128)S(1)}, u32[]{:S(2)}, u32[]{:S(2)}) async-start(s32[64,1,8]{2,1,0:T(1,128)} %broadcast_in_dim.86), calls=%async_computation | async-start | bytes 65536 | tf_op jit(solution)/shard_map/all_to_all | solution.py:20
  20.5 0.7 fusion.18
  21.3 6.7 %all-to-all-done = s32[64,1,8]{2,1,0:T(1,128)S(1)} async-done(((s32[64,1,8]{2,1,0:T(1,128)}), s32[64,1,8]{2,1,0:T(1,128)S(1)}, u32[]{:S(2)}, u32[]{:S(2)}) %all-to-all-start) | async-done | bytes 2080 | tf_op jit(solution)/shard_map/all_to_all | solution.py:20
  28.0 0.7 fusion.20
  29.4 1.1 convolution_convert_fusion.1
  30.5 2.1 broadcast_in_dim.93
  32.6 7.5 %all-to-all-start.1 = ((bf16[64,12,1536]{2,1,0:T(8,128)(2,1)}), bf16[64,12,1536]{2,1,0:T(8,128)(2,1)}, u32[]{:S(2)}, u32[]{:S(2)}) async-start(bf16[64,12,1536]{2,1,0:T(8,128)(2,1)} %bitcast.37), calls=%async_computation.1 | async-start | bytes 6291456 | tf_op jit(solution)/shard_map/all_to_all | solution.py:92
  40.6 0.7 compare_select_fusion.2
  41.3 0.7 iota_compare_fusion.7
  41.9 68.9 %all-to-all-done.1 = bf16[64,12,1536]{2,1,0:T(8,128)(2,1)} async-done(((bf16[64,12,1536]{2,1,0:T(8,128)(2,1)}), bf16[64,12,1536]{2,1,0:T(8,128)(2,1)}, u32[]{:S(2)}, u32[]{:S(2)}) %all-to-all-start.1) | async-done | bytes 2359328 | tf_op jit(solution)/shard_map/all_to_all | solution.py:92
  110.9 4.9 %reshape.343 = bf16[768,1536]{1,0:T(8,128)(2,1)} reshape(bf16[64,12,1536]{2,1,0:T(8,128)(2,1)} %all-to-all-done.1) | data formatting | bytes 4718592 | tf_op jit(solution)/shard_map/reshape | solution.py:95
  115.8 6.4 %gather_fusion = bf16[480,1536]{1,0:T(8,128)(2,1)} fusion(bf16[768,1536]{1,0:T(8,128)(2,1)} %reshape.343, s32[1024]{0:T(1024)S(1)} %pad_clamp_fusion.1), kind=kCustom, calls=%fused_computation | custom fusion | bytes 2951040 | tf_op jit(solution)/shard_map/jit(_take)/gather | solution.py:109
  122.1 2.8 select_select_fusion.1
  125.1 63.9 %all-gather.2.cloned.1.call-done = bf16[480,6144]{1,0:T(8,128)(2,1)} async-done(((bf16[480,1536]{1,0:T(8,128)(2,1)}), bf16[480,6144]{1,0:T(8,128)(2,1)}) %all-gather.2.cloned.1.call-update) | async-done | bytes 5898256 | tf_op jit(solution)/shard_map/all_gather | solution.py:111
  189.1 5.4 %fusion.3 = f32[480,256]{1,0:T(8,128)S(1)} fusion(bf16[480,6144]{1,0:T(8,128)(2,1)} %all-gather.2.cloned.1.call-done, bf16[1,6144,256]{2,1,0:T(8,128)(2,1)} %param.9), kind=kOutput, calls=%fused_computation.8 | convolution fusion | flops 1509949440 | bytes 9535488 | tf_op jit(solution)/shard_map/dot_general | solution.py:112
  194.5 0.8 copy-done.3
  195.3 1.7 fusion.8
  197.0 4.2 %convolution_convert_fusion = bf16[480,6144]{1,0:T(8,128)(2,1)} fusion(bf16[480,256]{1,0:T(8,128)(2,1)S(1)} %fusion.8, bf16[1,256,6144]{2,1,0:T(8,128)(2,1)S(1)} %copy-done), kind=kOutput, calls=%fused_computation.2 | convolution fusion | flops 1512898560 | bytes 9289728 | tf_op jit(solution)/shard_map/dot_general | solution.py:115
  202.1 63.3 %reduce-scatter.2.cloned.1.call-done = bf16[480,1536]{1,0:T(8,128)(2,1)} async-done(((bf16[480,6144]{1,0:T(8,128)(2,1)}), bf16[480,1536]{1,0:T(8,128)(2,1)}) %reduce-scatter.2.cloned.1.call-update) | async-done | bytes 1474576 | tf_op jit(solution)/shard_map/reduce_scatter | solution.py:116
  265.4 7.5 %gather_fusion.1 = bf16[768,1536]{1,0:T(8,128)(2,1)} fusion(bf16[480,1536]{1,0:T(8,128)(2,1)} %reduce-scatter.2.cloned.1.call-done, s32[1024]{0:T(1024)S(1)} %pad_clamp_fusion), kind=kCustom, calls=%fused_computation.1 | custom fusion | bytes 4721664 | tf_op jit(solution)/shard_map/jit(_take)/gather | solution.py:124
  272.8 4.8 %gather.12 = bf16[32,2,1,12,1536]{4,3,1,0,2:T(8,128)(2,1)} reshape(bf16[768,1536]{1,0:T(8,128)(2,1)} %gather_fusion.1) | data formatting | bytes 4718592 | tf_op jit(solution)/shard_map/jit(_take)/gather | solution.py:124
  277.6 2.2 select_select_fusion
  279.8 1.3 copy.61
  281.1 5.6 %all_to_all.20 = bf16[32,2,1,12,1536]{4,0,3,2,1:T(8,128)(2,1)S(1)} all-to-all(bf16[32,2,1,12,1536]{4,0,3,2,1:T(8,128)(2,1)S(1)} %copy.61), channel_id=1, replica_groups=mesh['expert_0'=4,'expert_1'=8,'expert_2'=2,'mp'=4] {'expert_2'}, dimensions={1} | all-to-all | bytes 4718592 | tf_op jit(solution)/shard_map/all_to_all | solution.py:39
  286.7 3.8 %copy.62 = bf16[32,2,1,12,1536]{4,1,3,2,0:T(2,128)(2,1)} copy(bf16[32,2,1,12,1536]{4,0,3,2,1:T(8,128)(2,1)S(1)} %all_to_all.20) | data formatting | bytes 4718592 | tf_op jit(solution)/shard_map/all_to_all | solution.py:39
  290.5 10.4 %all-to-all-start.3 = ((bf16[32,2,1,12,1536]{4,1,3,2,0:T(2,128)(2,1)}), bf16[32,2,1,12,1536]{4,1,3,2,0:T(2,128)(2,1)}, u32[]{:S(2)}, u32[]{:S(2)}) async-start(bf16[32,2,1,12,1536]{4,1,3,2,0:T(2,128)(2,1)} %copy.62), calls=%async_computation.4 | async-start | bytes 4718592 | tf_op jit(solution)/shard_map/all_to_all | solution.py:39
  301.4 55.5 %all-to-all-done.3 = bf16[32,2,1,12,1536]{4,1,3,2,0:T(2,128)(2,1)} async-done(((bf16[32,2,1,12,1536]{4,1,3,2,0:T(2,128)(2,1)}), bf16[32,2,1,12,1536]{4,1,3,2,0:T(2,128)(2,1)}, u32[]{:S(2)}, u32[]{:S(2)}) %all-to-all-start.3) | async-done | bytes 2359328 | tf_op jit(solution)/shard_map/all_to_all | solution.py:39
  356.9 8.2 %convert_reduce_fusion = f32[32,12,1536]{2,1,0:T(8,128)S(1)} fusion(bf16[32,2,1,12,1536]{4,1,3,2,0:T(2,128)(2,1)} %all-to-all-done.3), kind=kLoop, calls=%fused_computation.3 | loop fusion | flops 1769472 | bytes 4718592 | tf_op jit(solution)/shard_map/reduce_sum | solution.py:134
  365.1 1.1 bitcast_reduce_fusion
  366.3 2.0 reshape.344
  368.3 2.1 convolution_convert_fusion.2
  (52 shorter events, 3.7 us)
Async XLA Ops:
  6.5 190.5 %copy-start = (bf16[1,256,6144]{2,1,0:T(8,128)(2,1)S(1)}, bf16[1,256,6144]{2,1,0:T(8,128)(2,1)}, u32[]{:S(2)}) copy-start(bf16[1,256,6144]{2,1,0:T(8,128)(2,1)} %param.11) | copy-start | bytes 9437188
  8.3 19.7 %all-to-all-start = ((s32[64,1,8]{2,1,0:T(1,128)}), s32[64,1,8]{2,1,0:T(1,128)S(1)}, u32[]{:S(2)}, u32[]{:S(2)}) async-start(s32[64,1,8]{2,1,0:T(1,128)} %broadcast_in_dim.86), calls=%async_computation | async-start | bytes 65536 | tf_op jit(solution)/shard_map/all_to_all | solution.py:20
  32.6 78.3 %all-to-all-start.1 = ((bf16[64,12,1536]{2,1,0:T(8,128)(2,1)}), bf16[64,12,1536]{2,1,0:T(8,128)(2,1)}, u32[]{:S(2)}, u32[]{:S(2)}) async-start(bf16[64,12,1536]{2,1,0:T(8,128)(2,1)} %bitcast.37), calls=%async_computation.1 | async-start | bytes 6291456 | tf_op jit(solution)/shard_map/all_to_all | solution.py:92
  40.0 149.1 %all-gather.2.cloned.1.call-start = ((), (), s32[]{:S(2)}) async-start(), calls=%async_computation.5 | async-start | bytes 7372800 | tf_op jit(solution)/shard_map/all_gather | solution.py:111
  124.9 140.4 %reduce-scatter.2.cloned.1.call-start = ((), (), s32[]{:S(2)}) async-start(), calls=%async_computation.6 | async-start | bytes 7372800 | tf_op jit(solution)/shard_map/reduce_scatter | solution.py:116
  189.1 5.5 %copy-start.2 = (bf16[480,6144]{1,0:T(8,128)(2,1)S(1)}, bf16[480,6144]{1,0:T(8,128)(2,1)}, u32[]{:S(2)}) copy-start(bf16[480,6144]{1,0:T(8,128)(2,1)} %all-gather.2.cloned.1.call-done) | copy-start | bytes 17694724
  189.1 6.2 %copy-start.3 = (bf16[1,6144,256]{2,1,0:T(8,128)(2,1)S(1)}, bf16[1,6144,256]{2,1,0:T(8,128)(2,1)}, u32[]{:S(2)}) copy-start(bf16[1,6144,256]{2,1,0:T(8,128)(2,1)} %param.10) | copy-start | bytes 9437188
  290.5 10.4 %copy-start.1 = (f32[24,2]{0,1:T(2,128)S(1)}, f32[24,2]{0,1:T(2,128)}, u32[]{:S(2)}) copy-start(f32[24,2]{0,1:T(2,128)} %param.7) | copy-start | bytes 580
  290.5 66.4 %all-to-all-start.3 = ((bf16[32,2,1,12,1536]{4,1,3,2,0:T(2,128)(2,1)}), bf16[32,2,1,12,1536]{4,1,3,2,0:T(2,128)(2,1)}, u32[]{:S(2)}, u32[]{:S(2)}) async-start(bf16[32,2,1,12,1536]{4,1,3,2,0:T(2,128)(2,1)} %copy.62), calls=%async_computation.4 | async-start | bytes 4718592 | tf_op jit(solution)/shard_map/all_to_all | solution.py:39
Sparse Core Ops, SparseCore 0:
  125.0 63.9 all-gather.1
  201.4 63.9 reduce-scatter.1
where the time goes:
time: 378 us; the launch traced here: 377 us
  waiting for transfers between devices  258 us (68%)
  local copies, waits for them, and re-layouts  36.2 us (10%)
  starting transfers between devices  30.2 us (8%)
  other arithmetic  18.5 us (5%)
  matrix products  14.6 us (4%)
  between operations  13.7 us (4%)
  blocking collectives  5.63 us (1%)
    all_to_all x1, waiting for transfers between devices, local(): lax.all_to_all(pack_rows(pick_tokens, tokens, group_size), EXPERT, split_...  68.9 us
    all_gather x1, waiting for transfers between devices, local(): shard_piece = lax.all_gather(in_rows, 'mp', axis=1, tiled=True)  63.9 us
    reduce_scatter x1, waiting for transfers between devices, local(): lax.psum_scatter(part_sum.astype(jnp.bfloat16), 'mp', scatter_dimension=1...  63.3 us
    all_to_all x1, waiting for transfers between devices, exchange_in_order(): lax.all_to_all(pieces, axes[k], split_axis=k, concat_axis=k, tiled=True)  55.5 us
    gather x2, local copies, waits for them, and re-layouts, local(): jnp.take(reduced, back_idx, axis=0)  12.2 us
    all_to_all x1, starting transfers between devices, copy_for_each(): lax.all_to_all(jnp.broadcast_to(value[None], (size, *value.shape)), axis,...  12.2 us
    all_to_all x1, starting transfers between devices, exchange_in_order(): lax.all_to_all(pieces, axes[k], split_axis=k, concat_axis=k, tiled=True)  10.4 us
    reduce_sum x2, other arithmetic, local(): jnp.sum(returned.reshape(EXPERTS, group_size, most_rows, out_width).astyp...  9.32 us
  transfers between devices with their start and end apart: 5, of which 5 were waited for; matrix products, arithmetic and copies ran while one was open for 1% of the time, Pallas kernels for 0%

commit v1 on v0

--- a/solution.py
+++ b/solution.py
@@ -108,7 +108,9 @@
     in_rows = jnp.where(
         slot_valid[:, None], jnp.take(arrived_rows, fetch_idx, axis=0), jnp.zeros((), jnp.bfloat16)
     )
-    shard_piece = lax.all_gather(in_rows, "mp", axis=1, tiled=True)
+    shard_piece = jnp.concatenate(
+        lax.all_to_all(jnp.stack([in_rows] * lax.axis_size("mp")), "mp", 0, 0), axis=1
+    )
     gate_act = jnp.dot(shard_piece, gate_rows, preferred_element_type=jnp.float32)
     up_act = jnp.dot(shard_piece, up_rows, preferred_element_type=jnp.float32)
     hidden = activate(gate_act, up_act)

time: 378 us -> 376 us (level)
  blocking collectives: 5.63 us -> 77 us
  waiting for transfers between devices: 258 us -> 191 us
  matrix products: 14.6 us -> 10.8 us
    all_to_all x0 -> x1, blocking collectives: none -> 71.4 us  [local(): lax.all_to_all(jnp.stack([in_rows] * lax.axis_size('mp')), 'mp', 0, 0)]
    all_gather x1 -> x0, waiting for transfers between devices: 63.9 us -> none  [local(): shard_piece = lax.all_gather(in_rows, 'mp', axis=1, tiled=True)]
  transfers between devices with their start and end apart: 5 -> 4, of which waited for: 5 -> 4; matrix products, arithmetic and copies ran while one was open for 1% -> 1% of each run, Pallas kernels for 0% -> 0%
where the time goes in v1:
time: 376 us; the launch traced here: 375 us
  waiting for transfers between devices  191 us (51%)
  blocking collectives  77 us (20%)
  local copies, waits for them, and re-layouts  36.6 us (10%)
  starting transfers between devices  30 us (8%)
  other arithmetic  15.9 us (4%)
  between operations  13.7 us (4%)
  matrix products  10.8 us (3%)
    all_to_all x1, blocking collectives, local(): lax.all_to_all(jnp.stack([in_rows] * lax.axis_size('mp')), 'mp', 0, 0)  71.4 us
    all_to_all x1, waiting for transfers between devices, local(): lax.all_to_all(pack_rows(pick_tokens, tokens, group_size), EXPERT, split_...  68.9 us
    reduce_scatter x1, waiting for transfers between devices, local(): lax.psum_scatter(part_sum.astype(jnp.bfloat16), 'mp', scatter_dimension=1...  59.6 us
    all_to_all x1, waiting for transfers between devices, exchange_in_order(): lax.all_to_all(pieces, axes[k], split_axis=k, concat_axis=k, tiled=True)  55.5 us
    all_to_all x1, starting transfers between devices, copy_for_each(): lax.all_to_all(jnp.broadcast_to(value[None], (size, *value.shape)), axis,...  12.2 us
    gather x2, local copies, waits for them, and re-layouts, local(): jnp.take(reduced, back_idx, axis=0)  10.9 us
    all_to_all x1, starting transfers between devices, exchange_in_order(): lax.all_to_all(pieces, axes[k], split_axis=k, concat_axis=k, tiled=True)  10.4 us
    reduce_sum x2, other arithmetic, local(): jnp.sum(returned.reshape(EXPERTS, group_size, most_rows, out_width).astyp...  9.47 us
  transfers between devices with their start and end apart: 4, of which 4 were waited for; matrix products, arithmetic and copies ran while one was open for 1% of the time, Pallas kernels for 0%

profile of v1, /device:TPU:6, one launch (start us, length us, event | category | flops | bytes accessed | tf_op | source)
XLA Modules:
  0.0 374.9 jit_solution(11583925319145002250)
XLA Ops:
  6.5 0.9 copy.58
  8.3 12.2 %all-to-all-start = ((s32[64,1,8]{2,1,0:T(1,128)}), s32[64,1,8]{2,1,0:T(1,128)S(1)}, u32[]{:S(2)}, u32[]{:S(2)}) async-start(s32[64,1,8]{2,1,0:T(1,128)} %broadcast_in_dim.86), calls=%async_computation | async-start | bytes 65536 | tf_op jit(solution)/shard_map/all_to_all | solution.py:20
  20.5 0.7 fusion.18
  21.3 6.7 %all-to-all-done = s32[64,1,8]{2,1,0:T(1,128)S(1)} async-done(((s32[64,1,8]{2,1,0:T(1,128)}), s32[64,1,8]{2,1,0:T(1,128)S(1)}, u32[]{:S(2)}, u32[]{:S(2)}) %all-to-all-start) | async-done | bytes 2080 | tf_op jit(solution)/shard_map/all_to_all | solution.py:20
  28.0 0.7 fusion.20
  29.4 1.1 convolution_convert_fusion.1
  30.5 2.1 broadcast_in_dim.93
  32.6 7.5 %all-to-all-start.1 = ((bf16[64,12,1536]{2,1,0:T(8,128)(2,1)}), bf16[64,12,1536]{2,1,0:T(8,128)(2,1)}, u32[]{:S(2)}, u32[]{:S(2)}) async-start(bf16[64,12,1536]{2,1,0:T(8,128)(2,1)} %bitcast.41), calls=%async_computation.1 | async-start | bytes 6291456 | tf_op jit(solution)/shard_map/all_to_all | solution.py:92
  40.6 0.7 compare_select_fusion.2
  41.3 0.7 iota_compare_fusion.7
  41.9 68.9 %all-to-all-done.1 = bf16[64,12,1536]{2,1,0:T(8,128)(2,1)} async-done(((bf16[64,12,1536]{2,1,0:T(8,128)(2,1)}), bf16[64,12,1536]{2,1,0:T(8,128)(2,1)}, u32[]{:S(2)}, u32[]{:S(2)}) %all-to-all-start.1) | async-done | bytes 2359328 | tf_op jit(solution)/shard_map/all_to_all | solution.py:92
  110.9 4.9 %reshape.362 = bf16[768,1536]{1,0:T(8,128)(2,1)} reshape(bf16[64,12,1536]{2,1,0:T(8,128)(2,1)} %all-to-all-done.1) | data formatting | bytes 4718592 | tf_op jit(solution)/shard_map/reshape | solution.py:95
  115.8 6.3 %gather_fusion = bf16[480,1536]{1,0:T(8,128)(2,1)} fusion(bf16[768,1536]{1,0:T(8,128)(2,1)} %reshape.362, s32[1024]{0:T(1024)S(1)} %pad_clamp_fusion.1), kind=kCustom, calls=%fused_computation | custom fusion | bytes 2951040 | tf_op jit(solution)/shard_map/jit(_take)/gather | solution.py:109
  122.1 1.6 select_select_fusion.1
  124.2 71.4 %all_to_all.25 = bf16[4,480,1536]{2,1,0:T(8,128)(2,1)S(1)} all-to-all(bf16[4,480,1536]{2,1,0:T(8,128)(2,1)S(1)} %stack.2), channel_id=1, replica_groups=mesh['expert_0'=4,'expert_1'=8,'expert_2'=2,'mp'=4] {'mp'}, dimensions={0} | all-to-all | bytes 11796480 | tf_op jit(solution)/shard_map/all_to_all | solution.py:112
  195.6 0.8 copy.74
  196.5 1.0 copy-done.3
  197.5 1.7 fusion.3
  199.4 1.7 fusion.8
  201.1 4.2 %convolution_convert_fusion = bf16[480,6144]{1,0:T(8,128)(2,1)} fusion(bf16[480,256]{1,0:T(8,128)(2,1)S(1)} %fusion.8, bf16[1,256,6144]{2,1,0:T(8,128)(2,1)S(1)} %copy-done), kind=kOutput, calls=%fused_computation.2 | convolution fusion | flops 1512898560 | bytes 9289728 | tf_op jit(solution)/shard_map/dot_general | solution.py:117
  206.2 59.6 %reduce-scatter.2.cloned.1.call-done = bf16[480,1536]{1,0:T(8,128)(2,1)} async-done(((bf16[480,6144]{1,0:T(8,128)(2,1)}), bf16[480,1536]{1,0:T(8,128)(2,1)}) %reduce-scatter.2.cloned.1.call-update) | async-done | bytes 1474576 | tf_op jit(solution)/shard_map/reduce_scatter | solution.py:118
  265.8 7.5 %gather_fusion.1 = bf16[768,1536]{1,0:T(8,128)(2,1)} fusion(bf16[480,1536]{1,0:T(8,128)(2,1)} %reduce-scatter.2.cloned.1.call-done, s32[1024]{0:T(1024)S(1)} %pad_clamp_fusion), kind=kCustom, calls=%fused_computation.1 | custom fusion | bytes 4721664 | tf_op jit(solution)/shard_map/jit(_take)/gather | solution.py:126
  273.3 3.4 gather.12
  277.2 1.3 copy.66
  278.5 5.6 %all_to_all.26 = bf16[32,2,1,12,1536]{4,0,3,2,1:T(8,128)(2,1)S(1)} all-to-all(bf16[32,2,1,12,1536]{4,0,3,2,1:T(8,128)(2,1)S(1)} %copy.66), channel_id=1, replica_groups=mesh['expert_0'=4,'expert_1'=8,'expert_2'=2,'mp'=4] {'expert_2'}, dimensions={1} | all-to-all | bytes 4718592 | tf_op jit(solution)/shard_map/all_to_all | solution.py:39
  284.2 3.8 %copy.67 = bf16[32,2,1,12,1536]{4,1,3,2,0:T(2,128)(2,1)} copy(bf16[32,2,1,12,1536]{4,0,3,2,1:T(8,128)(2,1)S(1)} %all_to_all.26) | data formatting | bytes 4718592 | tf_op jit(solution)/shard_map/all_to_all | solution.py:39
  288.0 10.4 %all-to-all-start.4 = ((bf16[32,2,1,12,1536]{4,1,3,2,0:T(2,128)(2,1)}), bf16[32,2,1,12,1536]{4,1,3,2,0:T(2,128)(2,1)}, u32[]{:S(2)}, u32[]{:S(2)}) async-start(bf16[32,2,1,12,1536]{4,1,3,2,0:T(2,128)(2,1)} %copy.67), calls=%async_computation.5 | async-start | bytes 4718592 | tf_op jit(solution)/shard_map/all_to_all | solution.py:39
  298.9 55.5 %all-to-all-done.4 = bf16[32,2,1,12,1536]{4,1,3,2,0:T(2,128)(2,1)} async-done(((bf16[32,2,1,12,1536]{4,1,3,2,0:T(2,128)(2,1)}), bf16[32,2,1,12,1536]{4,1,3,2,0:T(2,128)(2,1)}, u32[]{:S(2)}, u32[]{:S(2)}) %all-to-all-start.4) | async-done | bytes 2359328 | tf_op jit(solution)/shard_map/all_to_all | solution.py:39
  354.4 8.3 %convert_reduce_fusion = f32[32,12,1536]{2,1,0:T(8,128)S(1)} fusion(bf16[32,2,1,12,1536]{4,1,3,2,0:T(2,128)(2,1)} %all-to-all-done.4), kind=kLoop, calls=%fused_computation.3 | loop fusion | flops 1769472 | bytes 4718592 | tf_op jit(solution)/shard_map/reduce_sum | solution.py:136
  362.8 1.1 bitcast_reduce_fusion
  363.9 2.0 reshape.365
  365.9 2.1 convolution_convert_fusion.2
  (54 shorter events, 4.7 us)
Async XLA Ops:
  6.5 194.6 %copy-start = (bf16[1,256,6144]{2,1,0:T(8,128)(2,1)S(1)}, bf16[1,256,6144]{2,1,0:T(8,128)(2,1)}, u32[]{:S(2)}) copy-start(bf16[1,256,6144]{2,1,0:T(8,128)(2,1)} %param.11) | copy-start | bytes 9437188
  8.3 19.7 %all-to-all-start = ((s32[64,1,8]{2,1,0:T(1,128)}), s32[64,1,8]{2,1,0:T(1,128)S(1)}, u32[]{:S(2)}, u32[]{:S(2)}) async-start(s32[64,1,8]{2,1,0:T(1,128)} %broadcast_in_dim.86), calls=%async_computation | async-start | bytes 65536 | tf_op jit(solution)/shard_map/all_to_all | solution.py:20
  32.6 78.3 %all-to-all-start.1 = ((bf16[64,12,1536]{2,1,0:T(8,128)(2,1)}), bf16[64,12,1536]{2,1,0:T(8,128)(2,1)}, u32[]{:S(2)}, u32[]{:S(2)}) async-start(bf16[64,12,1536]{2,1,0:T(8,128)(2,1)} %bitcast.41), calls=%async_computation.1 | async-start | bytes 6291456 | tf_op jit(solution)/shard_map/all_to_all | solution.py:92
  40.0 225.8 %reduce-scatter.2.cloned.1.call-start = ((), (), s32[]{:S(2)}) async-start(), calls=%async_computation.6 | async-start | bytes 7372800 | tf_op jit(solution)/shard_map/reduce_scatter | solution.py:118
  195.6 1.9 copy-start.3
  197.5 1.9 copy-start.4
  288.0 10.4 %copy-start.2 = (f32[24,2]{0,1:T(2,128)S(1)}, f32[24,2]{0,1:T(2,128)}, u32[]{:S(2)}) copy-start(f32[24,2]{0,1:T(2,128)} %param.7) | copy-start | bytes 580
  288.0 66.4 %all-to-all-start.4 = ((bf16[32,2,1,12,1536]{4,1,3,2,0:T(2,128)(2,1)}), bf16[32,2,1,12,1536]{4,1,3,2,0:T(2,128)(2,1)}, u32[]{:S(2)}, u32[]{:S(2)}) async-start(bf16[32,2,1,12,1536]{4,1,3,2,0:T(2,128)(2,1)} %copy.67), calls=%async_computation.5 | async-start | bytes 4718592 | tf_op jit(solution)/shard_map/all_to_all | solution.py:39
  354.4 13.6 %copy-start.1 = (bf16[1,256,6144]{2,1,0:T(8,128)(2,1)S(1)}, bf16[1,256,6144]{2,1,0:T(8,128)(2,1)}, u32[]{:S(2)}) copy-start(bf16[1,256,6144]{2,1,0:T(8,128)(2,1)} %param.11) | copy-start | bytes 9437188
Sparse Core Ops, SparseCore 0:
  205.5 60.2 reduce-scatter.1
